TPU v7x, 32 devices: a whole 2x2x4 slice. The times are simulated.
32 devices in a mesh: row: 8 (over z, y), col: 4 (over x, core).
Axes of the slice: x: 2, y: 2, z: 4, core: 2. Of those that a mesh axis runs over, the one named last changes fastest.
Arguments:
- points: float32 [16, 4096], P(None, ('col', 'row')), may hold values from -5 to 5
- inv_scales: float32 [16], replicated, may hold values from 0.1 to 0.4
- amplitude: float32 [1], replicated, may hold values from 0.5 to 2
- noise_var: float32 [1], replicated, may hold values from 0.3 to 1
- targets: float32 [8, 4096], P(None, ('col', 'row')), may hold values from -6 to 6
- initial: float32 [8, 4096], P(None, ('col', 'row')), may hold values from -3 to 3
- ritz_basis: float32 [64, 4096], P(None, ('col', 'row')), may hold values from -0.09375 to 0.09375
Outputs:
- solution: float32 [8, 4096], P(None, ('col', 'row'))
- residual: float32 [8, 4096], P(None, ('col', 'row'))
All inputs are finite; a program needn't handle non-finite values.
Results may differ from a plain program's by a relative error of at most 0.00065.
Values sent between devices are 32-bit elements; how exact they have to be, the bound alone decides.
A program may use at most 128 MiB of HBM per device.

v0:
```python
import jax
import jax.numpy as jnp
from jax import lax
from jax.sharding import PartitionSpec as P

ITERS = 1


HIGH = lax.Precision.HIGHEST


def kernel_tile(col_x, col_sq, row_x, row_sq, gain):
    cross_term = jnp.dot(col_x.T, row_x, precision=HIGH, preferred_element_type=jnp.float32)
    distance = jnp.maximum(col_sq[:, None] + row_sq[None, :] - 2.0 * cross_term, 0.0)
    return gain * jnp.exp(-0.5 * distance)


def coarse_solve(factor, rhs_block):
    middle = lax.linalg.triangular_solve(factor, rhs_block, left_side=True, lower=True)
    return lax.linalg.triangular_solve(factor, middle, left_side=True, lower=True, transpose_a=True)


def matmul(left, right):
    return jnp.dot(left, right, precision=HIGH, preferred_element_type=jnp.float32)


def local(points, inv_scales, amplitude, noise_var, targets, initial, ritz_basis):
    gain = amplitude[0]
    nugget = noise_var[0]
    all_x = lax.all_gather(points, ("row", "col"), axis=1, tiled=True) * inv_scales[:, None]
    all_sq = jnp.sum(all_x * all_x, axis=0)
    row_x = points * inv_scales[:, None]
    row_sq = jnp.sum(row_x * row_x, axis=0)

    def apply_operator(vectors):
        partial_value = matmul(
            lax.all_gather(vectors, ("row", "col"), axis=1, tiled=True),
            kernel_tile(all_x, all_sq, row_x, row_sq, gain),
        )
        return partial_value + nugget * vectors

    rhs_count = initial.shape[0]
    applied_all = apply_operator(jnp.concatenate([initial, ritz_basis], 0))
    ritz_image = applied_all[rhs_count:]
    first_residual = targets - applied_all[:rhs_count]
    coarse, projected = lax.psum(
        (matmul(ritz_basis, ritz_image.T), matmul(ritz_basis, first_residual.T)), ("row", "col")
    )
    coarse = 0.5 * (coarse + coarse.T)
    factor = jnp.linalg.cholesky(coarse)
    coarse_inverse = coarse_solve(factor, jnp.eye(coarse.shape[0], dtype=jnp.float32))
    amounts = matmul(coarse_inverse, projected)
    solution = initial + matmul(amounts.T, ritz_basis)
    residual = first_residual - matmul(amounts.T, ritz_image)

    def residual_stats(current):
        return lax.psum(
            (matmul(ritz_image, current.T), jnp.sum(current * current, axis=1)), ("row", "col")
        )

    against, sq_norm = residual_stats(residual)
    direction = residual - matmul(matmul(coarse_inverse, against).T, ritz_basis)

    def plain_step(step, state):
        solution, residual, direction, sq_norm = state
        applied = apply_operator(direction)
        curvature = lax.psum(jnp.sum(direction * applied, axis=1), ("row", "col"))
        step_size = sq_norm / curvature
        solution = solution + step_size[:, None] * direction
        residual = residual - step_size[:, None] * applied
        against, new_norm = residual_stats(residual)
        correction = matmul(matmul(coarse_inverse, against).T, ritz_basis)
        direction = residual + (new_norm / sq_norm)[:, None] * direction - correction
        return (solution, residual, direction, new_norm)

    solution, residual, direction, sq_norm = lax.fori_loop(
        0, ITERS, plain_step, (solution, residual, direction, sq_norm)
    )
    return (solution, residual)


def solution(mesh):
    placed = (
        P(None, ("col", "row")),
        P(),
        P(),
        P(),
        P(None, ("col", "row")),
        P(None, ("col", "row")),
        P(None, ("col", "row")),
    )
    return jax.shard_map(
        local,
        mesh=mesh,
        in_specs=placed,
        out_specs=(P(None, ("col", "row")), P(None, ("col", "row"))),
        check_vma=False,
    )
```

profile of v0, /device:TPU:0, one launch (start us, length us, event | category | flops | bytes accessed | tf_op | source)
XLA Modules:
  0.0 250.1 jit_solution(7430495101600024024)
XLA Ops:
  7.2 0.0 all-gather.2.cloned.1.call-start
  7.2 0.7 constant_dynamic-update-slice_fusion.1
  7.9 0.8 constant_dynamic-update-slice_fusion
  8.7 0.0 copy-start.1
  8.7 0.6 copy-done.1
  9.3 0.0 all-gather.2.cloned.1.call-update
  10.6 0.0 copy-start.2
  10.6 0.8 multiply_reduce_fusion.1
  11.4 44.4 %all_gather.11 = f32[16,4096]{1,0:T(8,128)S(1)} all-gather(f32[16,128]{1,0:T(8,128)} %param.7), channel_id=1, replica_groups=mesh['row'=8,'col'=4] {'row','col'}, dimensions={1}, use_global_device_ids=true | all-gather | bytes 270336 | tf_op jit(solution)/shard_map/all_gather | solution.py:30
  55.8 0.8 multiply_reduce_fusion
  56.5 4.8 %fusion.4 = f32[4096,128]{1,0:T(8,128)S(1)} fusion(f32[128]{0:T(128)S(1)} %multiply_reduce_fusion.1, f32[4096]{0:T(1024)S(1)} %multiply_reduce_fusion, f32[]{:T(128)} %bitcast.38, f32[16,4096]{1,0:T(8,128)S(1)} %all_gather.11, f32[16]{0:T(128)} %param.8, f32[16,128]{1,0:T(8,128)} %param.7), kind=kOutput, calls=%fused_computation.5 | convolution fusion | flops 103876608 | bytes 2384452 | tf_op jit(solution)/shard_map/dot_general | solution.py:13
  61.3 0.0 copy-start
  61.3 0.0 copy-start.3
  61.4 5.3 %all-gather.2.cloned.1.call-done = f32[72,4096]{1,0:T(8,128)} async-done(((f32[72,128]{1,0:T(8,128)}), f32[72,4096]{1,0:T(8,128)}) %all-gather.2.cloned.1.call-update) | async-done | bytes 1179664 | tf_op jit(solution)/shard_map/all_gather | solution.py:37
  66.6 0.0 copy-done.2
  66.6 2.7 %convolution_add_fusion = f32[72,128]{1,0:T(8,128)S(1)} fusion(f32[72,4096]{1,0:T(8,128)} %all-gather.2.cloned.1.call-done, f32[4096,128]{1,0:T(8,128)S(1)} %fusion.4, f32[72,128]{1,0:T(8,128)S(1)} %copy-done.2, f32[]{:T(128)} %bitcast.39), kind=kOutput, calls=%fused_computation.6 | convolution fusion | flops 453003264 | bytes 3350532 | tf_op jit(solution)/shard_map/dot_general | solution.py:24
  69.4 0.0 copy-done
  69.4 0.0 copy-start.4
  69.4 0.2 convolution_bitcast_fusion
  69.6 0.0 copy-done.3
  69.6 0.1 convolution_bitcast_fusion.1
  69.7 40.2 %all-reduce.1 = (f32[64,64]{0,1:T(8,128)S(1)}, f32[64,8]{0,1:T(8,128)S(1)}) all-reduce(f32[64,64]{0,1:T(8,128)S(1)} %convolution_bitcast_fusion, f32[64,8]{0,1:T(8,128)S(1)} %convolution_bitcast_fusion.1), channel_id=1, replica_groups=mesh['row'=8,'col'=4] {'row','col'}, use_global_device_ids=true, to_apply=%region_2.0 | all-reduce | flops 4608 | bytes 36864 | tf_op jit(solution)/shard_map/psum | solution.py:46
  110.0 0.1 copy.9
  110.1 0.1 copy.10
  110.2 5.8 %cholesky.17 = f32[64,64]{1,0:T(8,128)S(1)} custom-call(f32[64,64]{1,0:T(8,128)S(1)} %fusion.13), custom_call_target="Cholesky" | custom-call | tf_op jit(solution)/shard_map/jit(cholesky)/cholesky | solution.py:50
  116.0 0.6 compare_reduce_fusion
  116.7 0.7 fusion.8
  117.3 4.9 %custom-call.8 = f32[1,64,64]{1,2,0:T(8,128)S(1)} custom-call(f32[1,64,64]{2,1,0:T(8,128)S(1)} %fusion.8), custom_call_target="InvertDiagBlocksLowerTriangular" | custom-call | tf_op jit(solution)/shard_map/triangular_solve | solution.py:20
  122.2 0.2 fusion.11
  122.5 0.2 fusion.9
  122.6 0.1 fusion.21
  122.8 0.3 multiply_reduce_fusion.3
  123.1 0.2 fusion.15
  123.2 39.2 %psum.47 = f32[64,8]{1,0:T(8,128)S(1)} all-reduce(f32[64,8]{1,0:T(8,128)S(1)} %fusion.15), channel_id=1, replica_groups=mesh['row'=8,'col'=4] {'row','col'}, use_global_device_ids=true, to_apply=%region_8.0 | all-reduce | flops 512 | bytes 4096 | tf_op jit(solution)/shard_map/psum | solution.py:57
  162.4 0.2 fusion.22
  162.6 0.2 convolution_subtract_fusion
  162.8 41.0 %all_gather.12 = f32[8,4096]{1,0:T(8,128)S(1)} all-gather(f32[8,128]{1,0:T(8,128)S(1)} %convolution_subtract_fusion), channel_id=1, replica_groups=mesh['row'=8,'col'=4] {'row','col'}, dimensions={1}, use_global_device_ids=true | all-gather | bytes 135168 | tf_op jit(solution)/shard_map/while/body/eval_jaxpr/all_gather | solution.py:37
  203.7 1.2 multiply_reduce_fusion.2
  205.0 36.9 %all-reduce = (f32[8]{0:T(128)S(1)}, f32[8]{0:T(128)S(1)}) all-reduce(f32[8]{0:T(128)S(1)} %get-tuple-element.34, f32[8]{0:T(128)S(1)} %get-tuple-element.36), channel_id=1, replica_groups=mesh['row'=8,'col'=4] {'row','col'}, use_global_device_ids=true, to_apply=%region_7.8 | all-reduce | flops 16 | bytes 128 | tf_op jit(solution)/shard_map/psum | solution.py:57
  241.8 0.0 copy-done.4
  241.8 0.7 fusion.5
  242.6 0.7 multiply_subtract_fusion
  (4 shorter events, 0.1 us)
Async XLA Ops:
  7.2 59.5 %all-gather.2.cloned.1.call-start = ((), (), s32[]{:S(2)}) async-start(), calls=%async_computation | async-start | bytes 1216512 | tf_op jit(solution)/shard_map/all_gather | solution.py:37
  8.7 0.6 copy-start.1
  10.6 56.1 %copy-start.2 = (f32[72,128]{1,0:T(8,128)S(1)}, f32[72,128]{1,0:T(8,128)}, u32[]{:S(2)}) copy-start(f32[72,128]{1,0:T(8,128)} %copy-done.1) | copy-start | bytes 110596
  61.3 8.0 %copy-start = (f32[64,128]{1,0:T(8,128)S(1)}, f32[64,128]{1,0:T(8,128)}, u32[]{:S(2)}) copy-start(f32[64,128]{1,0:T(8,128)} %param.13) | copy-start | bytes 98308
  61.3 8.2 %copy-start.3 = (f32[8,128]{1,0:T(8,128)S(1)}, f32[8,128]{1,0:T(8,128)}, u32[]{:S(2)}) copy-start(f32[8,128]{1,0:T(8,128)} %param.11) | copy-start | bytes 12292
  69.4 172.4 %copy-start.4 = (f32[8,128]{1,0:T(8,128)S(1)}, f32[8,128]{1,0:T(8,128)}, u32[]{:S(2)}) copy-start(f32[8,128]{1,0:T(8,128)} %param.12) | copy-start | bytes 12292
Sparse Core Ops, SparseCore 0:
  10.8 55.7 all-gather.1
where the time goes:
time: 251 us; the launch traced here: 250 us
  blocking collectives  202 us (80%)
  between operations  15.5 us (6%)
  other arithmetic  14.3 us (6%)
  matrix products  11.2 us (4%)
  waiting for transfers between devices  5.28 us (2%)
    psum x2, blocking collectives, residual_stats(): lax.psum((matmul(ritz_image, current.T), jnp.sum(current * current, axis=...  76 us
    all_gather x1, blocking collectives, local(): lax.all_gather(points, ('row', 'col'), axis=1, tiled=True)  44.4 us
    all_gather x1, blocking collectives, apply_operator(): lax.all_gather(vectors, ('row', 'col'), axis=1, tiled=True)  41 us
    psum x1, blocking collectives, local(): lax.psum((matmul(ritz_basis, ritz_image.T), matmul(ritz_basis, first_resi...  40.2 us
    another operation x3, other arithmetic, local(): factor = jnp.linalg.cholesky(coarse)  6.52 us
    dot_general x10, matrix products, matmul(): jnp.dot(left, right, precision=HIGH, preferred_element_type=jnp.float32)  5.97 us
    another operation x2, other arithmetic, coarse_solve(): lax.linalg.triangular_solve(factor, middle, left_side=True, lower=True, t...  5.55 us
    all_gather x1, waiting for transfers between devices, apply_operator(): lax.all_gather(vectors, ('row', 'col'), axis=1, tiled=True)  5.27 us
  transfers between devices with their start and end apart: 1, of which 1 were waited for; matrix products, arithmetic and copies ran while one was open for 3% of the time, Pallas kernels for 0%

commit v1 on v0

v1 whole, which is shorter than its diff:
```python
import functools

import jax
import jax.numpy as jnp
from jax import lax
from jax.experimental import pallas as pl
from jax.experimental.pallas import tpu as pltpu
from jax.sharding import PartitionSpec as P

HIGH = lax.Precision.HIGHEST
MESH = pl.DeviceIdType.MESH
VMEM = pltpu.VMEM
SMEM = pltpu.SMEM
F32 = jnp.float32
BF16 = jnp.bfloat16


def dot(left, right, dims=((1,), (0,))):
    return lax.dot_general(left, right, (dims, ((), ())), precision=HIGH, preferred_element_type=F32)


def thirds(value):
    first = value.astype(BF16)
    rest = value - first.astype(F32)
    second = rest.astype(BF16)
    third = (rest - second.astype(F32)).astype(BF16)
    return first, second, third


def augmented(scaled, swap):
    feat, width = scaled.shape
    half = -0.5 * jnp.sum(scaled * scaled, axis=0, keepdims=True)
    at = lax.broadcasted_iota(jnp.int32, (16, width), 0)
    first, second = (1, 0) if swap else (0, 1)
    tail = jnp.where(at == first, half, jnp.where(at == second, 1.0, 0.0))
    return jnp.concatenate([scaled, tail], axis=0)


def kernel(
    rows, cols, pts, scl, amp, nug, tgt, x0, w, sol_out, res_out,
    xj, xi, vj, wi, kt, ts, rs1, pscr, r1, pfull, sscr, rj, ri, agscr, ag, ts2, dscr, rs2, cscr, cv,
    send, recv,
):
    r = lax.axis_index("row")
    c = lax.axis_index("col")
    block = pts.shape[1]
    ritz = w.shape[0]
    rhs = x0.shape[0]
    count = rows * cols
    me = r * cols + c

    def lanes(at):
        return pl.ds(pl.multiple_of(at * block, block), block)

    def row_peer(k):
        return lax.rem(r + k, rows), c

    def col_peer(k):
        return r, lax.rem(c + k, cols)

    def any_peer(k):
        return lax.rem(r + k // cols, rows), lax.rem(c + k % cols, cols)

    def each(n, body):
        if n <= 32:
            for k in range(1, n):
                body(k)
        else:
            lax.fori_loop(1, n, lambda k, carry: (body(k), carry)[1], 0)

    def start(phase, src, dst, peer):
        pltpu.make_async_remote_copy(
            src_ref=src, dst_ref=dst, send_sem=send.at[phase], recv_sem=recv.at[phase],
            device_id=peer, device_id_type=MESH,
        ).start()

    def drain(phase, ref):
        return pltpu.make_async_remote_copy(
            src_ref=ref, dst_ref=ref, send_sem=send.at[phase], recv_sem=recv.at[phase],
            device_id=(r, c), device_id_type=MESH,
        )

    barrier = pltpu.get_barrier_semaphore()

    def greet(k):
        pl.semaphore_signal(barrier, inc=1, device_id=any_peer(k), device_id_type=MESH)

    each(count, greet)
    xj[:, lanes(r)] = pts[...]
    xi[:, lanes(c)] = pts[...]
    vj[pl.ds(0, ritz), lanes(r)] = w[...]
    vj[pl.ds(ritz, rhs), lanes(r)] = x0[...]
    wi[:, lanes(c)] = w[...]
    pscr[...] = jnp.zeros_like(pscr)
    agscr[...] = jnp.zeros_like(agscr)
    pl.semaphore_wait(barrier, count - 1)

    each(rows, lambda k: start(0, pts, xj.at[:, lanes(r)], row_peer(k)))
    each(cols, lambda k: start(1, pts, xi.at[:, lanes(c)], col_peer(k)))
    each(rows, lambda k: start(2, w, vj.at[pl.ds(0, ritz), lanes(r)], row_peer(k)))
    each(cols, lambda k: start(3, w, wi.at[:, lanes(c)], col_peer(k)))
    each(rows, lambda k: start(4, x0, vj.at[pl.ds(ritz, rhs), lanes(r)], row_peer(k)))

    gain = amp[0]
    nugget = nug[0]
    feat = pts.shape[0]
    at = lax.broadcasted_iota(jnp.int32, (feat, 1), 0)
    scale = jnp.zeros((feat, 1), F32)
    for k in range(feat):
        scale = jnp.where(at == k, scl[k], scale)

    others_j = pl.ds(0, (rows - 1) * block)
    others_i = pl.ds(0, (cols - 1) * block)
    drain_xi = drain(1, xi.at[:, others_i])
    drain_xj = drain(0, xj.at[:, others_j])
    drain_xi.wait_recv()
    a, b, d = thirds(augmented(xi[...] * scale, True))
    right = jnp.concatenate([a, b, d, a, b, a], axis=0)
    drain_xj.wait_recv()
    a, b, d = thirds(augmented(xj[...] * scale, False))
    left = jnp.concatenate([a, a, a, b, b, d], axis=0)
    step = 2 * block
    for base in range(0, rows * block, step):
        half_distance = lax.dot_general(
            left[:, base:base + step], right, (((0,), (0,)), ((), ())), preferred_element_type=F32
        )
        kt[base:base + step, :] = gain * jnp.exp(jnp.minimum(half_distance, 0.0))

    drain_w = drain(2, vj.at[pl.ds(0, ritz), others_j])
    drain_x0 = drain(4, vj.at[pl.ds(ritz, rhs), others_j])
    drain_wi = drain(3, wi.at[:, others_i])
    drain_w.wait_recv()
    drain_x0.wait_recv()
    ts[...] = dot(vj[...], kt[...])
    ts[pl.ds(0, ritz), lanes(c)] += nugget * w[...]
    ts[pl.ds(ritz, rhs), lanes(c)] += nugget * x0[...] - tgt[...]
    each(cols, lambda k: start(5, ts.at[:, lanes(lax.rem(c + k, cols))], rs1.at[c], col_peer(k)))
    drain_wi.wait_recv()
    gram = dot(wi[...], ts[...], ((1,), (1,)))
    part = ritz // rows
    gram = jnp.concatenate([gram, jnp.zeros((ritz, block - ritz - rhs), F32)], axis=1)
    pscr[...] = gram.reshape(rows, part, block)

    def send_part(k):
        peer = any_peer(k)
        start(6, pscr.at[peer[0]], r1.at[me], peer)

    each(count, send_part)
    r1[me] = pscr[r]
    rs1[c] = ts[:, lanes(c)]
    drain_r1 = drain(6, r1.at[pl.ds(0, count - 1)])
    drain_r1.wait_recv()
    mine = jnp.sum(r1[...], axis=0)
    sscr[...] = mine
    each(rows, lambda k: start(7, sscr, pfull.at[r], row_peer(k)))
    pfull[r] = mine
    drain_rs1 = drain(5, rs1.at[pl.ds(0, cols - 1)])
    drain_rs1.wait_recv()
    own = jnp.sum(rs1[...], axis=0)
    image = own[:ritz]
    drain_pf = drain(7, pfull.at[pl.ds(0, rows - 1)])
    drain_pf.wait_recv()
    full = pfull[...].reshape(ritz, block)

    lane = lax.broadcasted_iota(jnp.int32, (8, block), 1)
    lane_row = lax.broadcasted_iota(jnp.int32, (1, block), 1)
    sub = lax.broadcasted_iota(jnp.int32, (8, block), 0)
    pad = jnp.zeros((block - ritz, block), F32)
    flipped = jnp.concatenate([full, pad], axis=0).T[:ritz]
    tiles = []
    for i in range(ritz // 8):
        top = full[8 * i:8 * i + 8]
        tiles.append(jnp.where(lane < ritz, 0.5 * (top + flipped[8 * i:8 * i + 8]), top))
    for k in range(ritz):
        hold, inner = divmod(k, 8)
        pivot_row = tiles[hold][inner:inner + 1]
        inverse = 1.0 / pivot_row[:, k:k + 1]
        pivot_row = jnp.where(lane_row == k, 1.0, pivot_row) * inverse
        for i in range(ritz // 8):
            column = jnp.broadcast_to(tiles[i][:, k:k + 1], (8, block))
            kept = jnp.where(lane == k, 0.0, tiles[i])
            if i == hold:
                column = jnp.where(sub == inner, -1.0, column)
                kept = jnp.where(sub == inner, 0.0, kept)
            tiles[i] = kept - column * pivot_row
    turned = jnp.concatenate(tiles + [pad], axis=0).T
    inverse = turned[:ritz, :ritz]
    amounts = -turned[ritz:ritz + rhs, :ritz]
    moved = dot(amounts, jnp.concatenate([image, w[...]], axis=1))
    residual = -own[ritz:] - moved[:, :block]
    iterate = x0[...] + moved[:, block:]
    agscr[...] = jnp.concatenate(
        [dot(residual, image, ((1,), (1,))), jnp.zeros((rhs, block - ritz), F32)], axis=1
    )
    res_out[...] = residual
    rj[:, lanes(r)] = residual
    ri[:, lanes(c)] = residual
    each(count, lambda k: start(10, agscr, ag.at[me], any_peer(k)))
    each(rows, lambda k: start(8, res_out, rj.at[:, lanes(r)], row_peer(k)))
    each(cols, lambda k: start(9, res_out, ri.at[:, lanes(c)], col_peer(k)))
    ag[me] = agscr[...]
    drain_ag = drain(10, ag.at[pl.ds(0, count - 1)])
    drain_rj = drain(8, rj.at[:, others_j])
    drain_ri = drain(9, ri.at[:, others_i])
    drain_ag.wait_recv()
    against = jnp.sum(ag[...], axis=0)[:, :ritz]
    weights = dot(against, inverse)
    drain_rj.wait_recv()
    direction_j = rj[...] - dot(weights, vj[pl.ds(0, ritz), :])
    drain_ri.wait_recv()
    direction_i = ri[...] - dot(weights, wi[...])
    dscr[...] = direction_i
    direction = dscr[:, lanes(c)]
    applied_i = dot(direction_j, kt[...])
    ts2[...] = applied_i
    ts2[:, lanes(c)] += nugget * direction
    each(cols, lambda k: start(11, ts2.at[:, lanes(lax.rem(c + k, cols))], rs2.at[c], col_peer(k)))
    curve = jnp.sum(ts2[...] * direction_i, axis=1, keepdims=True)
    squares = jnp.sum(residual * residual, axis=1, keepdims=True)
    lane = lax.broadcasted_iota(jnp.int32, (rhs, block), 1)
    sub = lax.broadcasted_iota(jnp.int32, (rhs, block), 0)
    cscr[...] = jnp.sum(
        jnp.where(lane == sub, curve, jnp.where(lane == sub + rhs, squares, 0.0)), axis=0, keepdims=True
    )
    each(count, lambda k: start(12, cscr, cv.at[me], any_peer(k)))
    cv[me] = cscr[...]
    rs2[c] = ts2[:, lanes(c)]
    drain_rs2 = drain(11, rs2.at[pl.ds(0, cols - 1)])
    drain_cv = drain(12, cv.at[pl.ds(0, count - 1)])
    drain_rs2.wait_recv()
    applied = jnp.sum(rs2[...], axis=0)
    drain_cv.wait_recv()
    totals = jnp.broadcast_to(jnp.sum(cv[...], axis=0), (rhs, block))
    curve = jnp.sum(jnp.where(lane == sub, totals, 0.0), axis=1, keepdims=True)
    squares = jnp.sum(jnp.where(lane == sub + rhs, totals, 0.0), axis=1, keepdims=True)
    step_size = squares / curve
    sol_out[...] = iterate + step_size * direction
    drain_rj.wait_send()
    drain_ri.wait_send()
    res_out[...] = residual - step_size * applied
    for item in (drain_xj, drain_xi, drain_w, drain_wi, drain_x0, drain_rs1, drain_r1, drain_pf,
                 drain_ag, drain_rs2, drain_cv):
        item.wait_send()


def local(rows, cols, points, inv_scales, amplitude, noise_var, targets, initial, ritz_basis):
    feat, block = points.shape
    rhs = initial.shape[0]
    ritz = ritz_basis.shape[0]
    count = rows * cols
    vectors = rhs + ritz
    part = ritz // rows
    scratch = [
        VMEM((feat, rows * block), F32),
        VMEM((feat, cols * block), F32),
        VMEM((vectors, rows * block), F32),
        VMEM((ritz, cols * block), F32),
        VMEM((rows * block, cols * block), F32),
        VMEM((vectors, cols * block), F32),
        VMEM((cols, vectors, block), F32),
        VMEM((rows, part, block), F32),
        VMEM((count, part, block), F32),
        VMEM((rows, part, block), F32),
        VMEM((part, block), F32),
        VMEM((rhs, rows * block), F32),
        VMEM((rhs, cols * block), F32),
        VMEM((rhs, block), F32),
        VMEM((count, rhs, block), F32),
        VMEM((rhs, cols * block), F32),
        VMEM((rhs, cols * block), F32),
        VMEM((cols, rhs, block), F32),
        VMEM((1, block), F32),
        VMEM((count, 1, block), F32),
        pltpu.SemaphoreType.DMA((13,)),
        pltpu.SemaphoreType.DMA((13,)),
    ]
    vmem = pl.BlockSpec(memory_space=VMEM)
    smem = pl.BlockSpec(memory_space=SMEM)
    return pl.pallas_call(
        functools.partial(kernel, rows, cols),
        out_shape=[jax.ShapeDtypeStruct((rhs, block), F32)] * 2,
        in_specs=[vmem, smem, smem, smem, vmem, vmem, vmem],
        out_specs=[vmem, vmem],
        scratch_shapes=scratch,
        compiler_params=pltpu.CompilerParams(
            collective_id=0, has_side_effects=True, vmem_limit_bytes=48 * 1024 * 1024
        ),
        name="deflated_cg",
    )(points, inv_scales, amplitude, noise_var, targets, initial, ritz_basis)


def solution(mesh):
    spread = P(None, ("col", "row"))
    return jax.shard_map(
        functools.partial(local, mesh.shape["row"], mesh.shape["col"]),
        mesh=mesh,
        in_specs=(spread, P(), P(), P(), spread, spread, spread),
        out_specs=(spread, spread),
        check_vma=False,
    )
```

time: 251 us -> 51.7 us (0.21)
  blocking collectives: 202 us -> 0 us
  Pallas kernels: 0 us -> 45.4 us
  other arithmetic: 14.3 us -> 0 us
  between operations: 15.5 us -> 1.97 us
  matrix products: 11.2 us -> 0 us
  waiting for transfers between devices: 5.28 us -> 0 us
    psum x3 -> x0, blocking collectives: 116 us -> none  [the longest x2 76 us: residual_stats(): lax.psum((matmul(ritz_image, current.T), jnp.sum(current * current, axis=...]
    all_gather x2 -> x0, blocking collectives: 85.3 us -> none  [the longest x1 44.4 us: local(): lax.all_gather(points, ('row', 'col'), axis=1, tiled=True)]
    pallas_call x0 -> x1, Pallas kernels: none -> 45.4 us  [local(): pl.pallas_call(functools.partial(kernel, rows, cols), out_shape=[jax.Shap...]
    another operation x5 -> x0, other arithmetic: 12.1 us -> none  [the longest x3 6.52 us: local(): factor = jnp.linalg.cholesky(coarse)]
    dot_general x11 -> x0, matrix products: 10.8 us -> none  [the longest x10 5.97 us: matmul(): jnp.dot(left, right, precision=HIGH, preferred_element_type=jnp.float32)]
    all_gather x1 -> x0, waiting for transfers between devices: 5.27 us -> none  [apply_operator(): lax.all_gather(vectors, ('row', 'col'), axis=1, tiled=True)]
    unnamed x11 -> x12, local copies, waits for them, and re-layouts: 1.31 us -> 4.01 us
  transfers between devices with their start and end apart: 1 -> 0, of which waited for: 1 -> 0; matrix products, arithmetic and copies ran while one was open for 3% -> 0% of each run, Pallas kernels for 0% -> 0%
where the time goes in v1:
time: 51.7 us; the launch traced here: 51.4 us
  Pallas kernels  45.4 us (88%)
  local copies, waits for them, and re-layouts  4.01 us (8%)
  between operations  1.97 us (4%)
    pallas_call x1, Pallas kernels, local(): pl.pallas_call(functools.partial(kernel, rows, cols), out_shape=[jax.Shap...  45.4 us
    unnamed x12, local copies, waits for them, and re-layouts  4.01 us

profile of v1, /device:TPU:0, one launch (start us, length us, event | category | flops | bytes accessed | tf_op | source)
XLA Modules:
  0.0 51.4 jit_solution(670427897123416185)
XLA Ops:
  1.3 0.0 copy-start.4
  1.9 0.0 copy-done.4
  2.0 0.0 copy-start
  2.0 0.7 %copy-done = f32[64,128]{1,0:T(8,128)S(1)} copy-done((f32[64,128]{1,0:T(8,128)S(1)}, f32[64,128]{1,0:T(8,128)}, u32[]{:S(2)}) %copy-start) | copy-done | bytes 32792
  2.7 0.0 copy-start.1
  2.7 0.7 %copy-done.1 = f32[16,128]{1,0:T(8,128)S(1)} copy-done((f32[16,128]{1,0:T(8,128)S(1)}, f32[16,128]{1,0:T(8,128)}, u32[]{:S(2)}) %copy-start.1) | copy-done | bytes 8216
  3.4 0.0 copy-start.2
  3.4 0.7 %copy-done.2 = f32[8,128]{1,0:T(8,128)S(1)} copy-done((f32[8,128]{1,0:T(8,128)S(1)}, f32[8,128]{1,0:T(8,128)}, u32[]{:S(2)}) %copy-start.2) | copy-done | bytes 4120
  4.1 0.0 copy-start.3
  4.1 0.7 %copy-done.3 = f32[8,128]{1,0:T(8,128)S(1)} copy-done((f32[8,128]{1,0:T(8,128)S(1)}, f32[8,128]{1,0:T(8,128)}, u32[]{:S(2)}) %copy-start.3) | copy-done | bytes 4120
  4.8 45.4 %deflated_cg.1 = (f32[8,128]{1,0:T(8,128)S(1)}, f32[8,128]{1,0:T(8,128)S(1)}) custom-call(f32[16,128]{1,0:T(8,128)S(1)} %copy-done.1, f32[16]{0:T(128)S(1)} %copy-done.4, f32[1]{0:T(128)S(6)} %copy.11.amp, f32[1]{0:T(128)S(6)} %copy.12.nug, f32[8,128]{1,0:T(8,128)S(1)} %copy-done.2, f32[8,128]{1,0:T(8,128)S(1)} %copy-done.3, f32[64,128]{1,0:T(8,128)S(1)} %copy-done), custom_call_target="tpu_custom_call" | custom-call | tf_op jit(solution)/shard_map/deflated_cg/pallas_call | solution.py:279
  50.2 0.6 %copy.13 = f32[8,128]{1,0:T(8,128)} copy(f32[8,128]{1,0:T(8,128)S(1)} %get-tuple-element.4) | data formatting | bytes 8192
  50.8 0.6 %copy.14 = f32[8,128]{1,0:T(8,128)} copy(f32[8,128]{1,0:T(8,128)S(1)} %get-tuple-element.5) | data formatting | bytes 8192
Async XLA Ops:
  1.3 0.7 %copy-start.4 = (f32[16]{0:T(128)S(1)}, f32[16]{0:T(128)}, u32[]{:S(2)}) copy-start(f32[16]{0:T(128)} %scl.1) | copy-start | bytes 196
  2.0 0.8 %copy-start = (f32[64,128]{1,0:T(8,128)S(1)}, f32[64,128]{1,0:T(8,128)}, u32[]{:S(2)}) copy-start(f32[64,128]{1,0:T(8,128)} %w.1) | copy-start | bytes 98308
  2.7 0.7 %copy-start.1 = (f32[16,128]{1,0:T(8,128)S(1)}, f32[16,128]{1,0:T(8,128)}, u32[]{:S(2)}) copy-start(f32[16,128]{1,0:T(8,128)} %pts.1) | copy-start | bytes 24580
  3.4 0.7 %copy-start.2 = (f32[8,128]{1,0:T(8,128)S(1)}, f32[8,128]{1,0:T(8,128)}, u32[]{:S(2)}) copy-start(f32[8,128]{1,0:T(8,128)} %tgt.1) | copy-start | bytes 12292
  4.1 0.7 %copy-start.3 = (f32[8,128]{1,0:T(8,128)S(1)}, f32[8,128]{1,0:T(8,128)}, u32[]{:S(2)}) copy-start(f32[8,128]{1,0:T(8,128)} %x0.1) | copy-start | bytes 12292

commit v2 on v1

--- a/solution.py
+++ b/solution.py
@@ -37,29 +37,43 @@
 
 
 def kernel(
-    rows, cols, pts, scl, amp, nug, tgt, x0, w, sol_out, res_out,
+    high, low, cols, pts_in, scl_in, amp_in, nug_in, tgt_in, x0_in, w_in, out,
+    pts, scl, amp, nug, tgt, x0, w, res,
     xj, xi, vj, wi, kt, ts, rs1, pscr, r1, pfull, sscr, rj, ri, agscr, ag, ts2, dscr, rs2, cscr, cv,
-    send, recv,
+    loads, send, recv,
 ):
-    r = lax.axis_index("row")
-    c = lax.axis_index("col")
+    rows = low * cols
+    me = lax.axis_index("row") * cols + lax.axis_index("col")
+    h = me // rows
+    j = lax.rem(me, rows)
     block = pts.shape[1]
     ritz = w.shape[0]
     rhs = x0.shape[0]
-    count = rows * cols
-    me = r * cols + c
+    count = high * rows
+
+    fetches = [
+        pltpu.make_async_copy(src, dst, loads.at[k])
+        for k, (src, dst) in enumerate(
+            ((pts_in, pts), (w_in, w), (x0_in, x0), (tgt_in, tgt), (scl_in, scl), (amp_in, amp), (nug_in, nug))
+        )
+    ]
+    for fetch in fetches:
+        fetch.start()
 
     def lanes(at):
         return pl.ds(pl.multiple_of(at * block, block), block)
 
+    def place(flat):
+        return flat // cols, lax.rem(flat, cols)
+
     def row_peer(k):
-        return lax.rem(r + k, rows), c
+        return place(h * rows + lax.rem(j + k, rows))
 
     def col_peer(k):
-        return r, lax.rem(c + k, cols)
+        return place(lax.rem(h + k, high) * rows + j)
 
     def any_peer(k):
-        return lax.rem(r + k // cols, rows), lax.rem(c + k % cols, cols)
+        return place(lax.rem(me + k, count))
 
     def each(n, body):
         if n <= 32:
@@ -77,29 +91,32 @@
     def drain(phase, ref):
         return pltpu.make_async_remote_copy(
             src_ref=ref, dst_ref=ref, send_sem=send.at[phase], recv_sem=recv.at[phase],
-            device_id=(r, c), device_id_type=MESH,
+            device_id=place(me), device_id_type=MESH,
         )
 
     barrier = pltpu.get_barrier_semaphore()
 
-    def greet(k):
-        pl.semaphore_signal(barrier, inc=1, device_id=any_peer(k), device_id_type=MESH)
-
-    each(count, greet)
-    xj[:, lanes(r)] = pts[...]
-    xi[:, lanes(c)] = pts[...]
-    vj[pl.ds(0, ritz), lanes(r)] = w[...]
-    vj[pl.ds(ritz, rhs), lanes(r)] = x0[...]
-    wi[:, lanes(c)] = w[...]
+    def greet(peer):
+        pl.semaphore_signal(barrier, inc=1, device_id=peer, device_id_type=MESH)
+
+    each(high, lambda k: greet(col_peer(k)))
+    each(rows, lambda k: greet(row_peer(k)))
     pscr[...] = jnp.zeros_like(pscr)
     agscr[...] = jnp.zeros_like(agscr)
-    pl.semaphore_wait(barrier, count - 1)
-
-    each(rows, lambda k: start(0, pts, xj.at[:, lanes(r)], row_peer(k)))
-    each(cols, lambda k: start(1, pts, xi.at[:, lanes(c)], col_peer(k)))
-    each(rows, lambda k: start(2, w, vj.at[pl.ds(0, ritz), lanes(r)], row_peer(k)))
-    each(cols, lambda k: start(3, w, wi.at[:, lanes(c)], col_peer(k)))
-    each(rows, lambda k: start(4, x0, vj.at[pl.ds(ritz, rhs), lanes(r)], row_peer(k)))
+    for fetch in fetches:
+        fetch.wait()
+    xj[:, lanes(j)] = pts[...]
+    xi[:, lanes(h)] = pts[...]
+    vj[pl.ds(0, ritz), lanes(j)] = w[...]
+    vj[pl.ds(ritz, rhs), lanes(j)] = x0[...]
+    wi[:, lanes(h)] = w[...]
+    pl.semaphore_wait(barrier, high + rows - 2)
+
+    each(rows, lambda k: start(0, pts, xj.at[:, lanes(j)], row_peer(k)))
+    each(high, lambda k: start(1, pts, xi.at[:, lanes(h)], col_peer(k)))
+    each(rows, lambda k: start(2, w, vj.at[pl.ds(0, ritz), lanes(j)], row_peer(k)))
+    each(high, lambda k: start(3, w, wi.at[:, lanes(h)], col_peer(k)))
+    each(rows, lambda k: start(4, x0, vj.at[pl.ds(ritz, rhs), lanes(j)], row_peer(k)))
 
     gain = amp[0]
     nugget = nug[0]
@@ -110,7 +127,7 @@
         scale = jnp.where(at == k, scl[k], scale)
 
     others_j = pl.ds(0, (rows - 1) * block)
-    others_i = pl.ds(0, (cols - 1) * block)
+    others_i = pl.ds(0, (high - 1) * block)
     drain_xi = drain(1, xi.at[:, others_i])
     drain_xj = drain(0, xj.at[:, others_j])
     drain_xi.wait_recv()
@@ -132,9 +149,9 @@
     drain_w.wait_recv()
     drain_x0.wait_recv()
     ts[...] = dot(vj[...], kt[...])
-    ts[pl.ds(0, ritz), lanes(c)] += nugget * w[...]
-    ts[pl.ds(ritz, rhs), lanes(c)] += nugget * x0[...] - tgt[...]
-    each(cols, lambda k: start(5, ts.at[:, lanes(lax.rem(c + k, cols))], rs1.at[c], col_peer(k)))
+    ts[pl.ds(0, ritz), lanes(h)] += nugget * w[...]
+    ts[pl.ds(ritz, rhs), lanes(h)] += nugget * x0[...] - tgt[...]
+    each(high, lambda k: start(5, ts.at[:, lanes(lax.rem(h + k, high))], rs1.at[h], col_peer(k)))
     drain_wi.wait_recv()
     gram = dot(wi[...], ts[...], ((1,), (1,)))
     part = ritz // rows
@@ -142,19 +159,18 @@
     pscr[...] = gram.reshape(rows, part, block)
 
     def send_part(k):
-        peer = any_peer(k)
-        start(6, pscr.at[peer[0]], r1.at[me], peer)
+        start(6, pscr.at[lax.rem(j + k, rows)], r1.at[me], any_peer(k))
 
     each(count, send_part)
-    r1[me] = pscr[r]
-    rs1[c] = ts[:, lanes(c)]
+    r1[me] = pscr[j]
+    rs1[h] = ts[:, lanes(h)]
     drain_r1 = drain(6, r1.at[pl.ds(0, count - 1)])
     drain_r1.wait_recv()
     mine = jnp.sum(r1[...], axis=0)
     sscr[...] = mine
-    each(rows, lambda k: start(7, sscr, pfull.at[r], row_peer(k)))
-    pfull[r] = mine
-    drain_rs1 = drain(5, rs1.at[pl.ds(0, cols - 1)])
+    each(rows, lambda k: start(7, sscr, pfull.at[j], row_peer(k)))
+    pfull[j] = mine
+    drain_rs1 = drain(5, rs1.at[pl.ds(0, high - 1)])
     drain_rs1.wait_recv()
     own = jnp.sum(rs1[...], axis=0)
     image = own[:ritz]
@@ -192,12 +208,12 @@
     agscr[...] = jnp.concatenate(
         [dot(residual, image, ((1,), (1,))), jnp.zeros((rhs, block - ritz), F32)], axis=1
     )
-    res_out[...] = residual
-    rj[:, lanes(r)] = residual
-    ri[:, lanes(c)] = residual
+    res[...] = residual
+    rj[:, lanes(j)] = residual
+    ri[:, lanes(h)] = residual
     each(count, lambda k: start(10, agscr, ag.at[me], any_peer(k)))
-    each(rows, lambda k: start(8, res_out, rj.at[:, lanes(r)], row_peer(k)))
-    each(cols, lambda k: start(9, res_out, ri.at[:, lanes(c)], col_peer(k)))
+    each(rows, lambda k: start(8, res, rj.at[:, lanes(j)], row_peer(k)))
+    each(high, lambda k: start(9, res, ri.at[:, lanes(h)], col_peer(k)))
     ag[me] = agscr[...]
     drain_ag = drain(10, ag.at[pl.ds(0, count - 1)])
     drain_rj = drain(8, rj.at[:, others_j])
@@ -210,11 +226,11 @@
     drain_ri.wait_recv()
     direction_i = ri[...] - dot(weights, wi[...])
     dscr[...] = direction_i
-    direction = dscr[:, lanes(c)]
+    direction = dscr[:, lanes(h)]
     applied_i = dot(direction_j, kt[...])
     ts2[...] = applied_i
-    ts2[:, lanes(c)] += nugget * direction
-    each(cols, lambda k: start(11, ts2.at[:, lanes(lax.rem(c + k, cols))], rs2.at[c], col_peer(k)))
+    ts2[:, lanes(h)] += nugget * direction
+    each(high, lambda k: start(11, ts2.at[:, lanes(lax.rem(h + k, high))], rs2.at[h], col_peer(k)))
     curve = jnp.sum(ts2[...] * direction_i, axis=1, keepdims=True)
     squares = jnp.sum(residual * residual, axis=1, keepdims=True)
     lane = lax.broadcasted_iota(jnp.int32, (rhs, block), 1)
@@ -224,8 +240,8 @@
     )
     each(count, lambda k: start(12, cscr, cv.at[me], any_peer(k)))
     cv[me] = cscr[...]
-    rs2[c] = ts2[:, lanes(c)]
-    drain_rs2 = drain(11, rs2.at[pl.ds(0, cols - 1)])
+    rs2[h] = ts2[:, lanes(h)]
+    drain_rs2 = drain(11, rs2.at[pl.ds(0, high - 1)])
     drain_cv = drain(12, cv.at[pl.ds(0, count - 1)])
     drain_rs2.wait_recv()
     applied = jnp.sum(rs2[...], axis=0)
@@ -234,65 +250,75 @@
     curve = jnp.sum(jnp.where(lane == sub, totals, 0.0), axis=1, keepdims=True)
     squares = jnp.sum(jnp.where(lane == sub + rhs, totals, 0.0), axis=1, keepdims=True)
     step_size = squares / curve
-    sol_out[...] = iterate + step_size * direction
-    drain_rj.wait_send()
-    drain_ri.wait_send()
-    res_out[...] = residual - step_size * applied
-    for item in (drain_xj, drain_xi, drain_w, drain_wi, drain_x0, drain_rs1, drain_r1, drain_pf,
+    out[pl.ds(0, rhs)] = iterate + step_size * direction
+    out[pl.ds(rhs, rhs)] = residual - step_size * applied
+    for item in (drain_rj, drain_ri, drain_xj, drain_xi, drain_w, drain_wi, drain_x0, drain_rs1, drain_r1, drain_pf,
                  drain_ag, drain_rs2, drain_cv):
         item.wait_send()
 
 
-def local(rows, cols, points, inv_scales, amplitude, noise_var, targets, initial, ritz_basis):
+def local(high, low, cols, points, inv_scales, amplitude, noise_var, targets, initial, ritz_basis):
     feat, block = points.shape
     rhs = initial.shape[0]
     ritz = ritz_basis.shape[0]
-    count = rows * cols
+    rows = low * cols
+    count = high * rows
     vectors = rhs + ritz
     part = ritz // rows
     scratch = [
+        VMEM((feat, block), F32),
+        SMEM((feat,), F32),
+        SMEM((1,), F32),
+        SMEM((1,), F32),
+        VMEM((rhs, block), F32),
+        VMEM((rhs, block), F32),
+        VMEM((ritz, block), F32),
+        VMEM((rhs, block), F32),
         VMEM((feat, rows * block), F32),
-        VMEM((feat, cols * block), F32),
+        VMEM((feat, high * block), F32),
         VMEM((vectors, rows * block), F32),
-        VMEM((ritz, cols * block), F32),
-        VMEM((rows * block, cols * block), F32),
-        VMEM((vectors, cols * block), F32),
-        VMEM((cols, vectors, block), F32),
+        VMEM((ritz, high * block), F32),
+        VMEM((rows * block, high * block), F32),
+        VMEM((vectors, high * block), F32),
+        VMEM((high, vectors, block), F32),
         VMEM((rows, part, block), F32),
         VMEM((count, part, block), F32),
         VMEM((rows, part, block), F32),
         VMEM((part, block), F32),
         VMEM((rhs, rows * block), F32),
-        VMEM((rhs, cols * block), F32),
+        VMEM((rhs, high * block), F32),
         VMEM((rhs, block), F32),
         VMEM((count, rhs, block), F32),
-        VMEM((rhs, cols * block), F32),
-        VMEM((rhs, cols * block), F32),
-        VMEM((cols, rhs, block), F32),
+        VMEM((rhs, high * block), F32),
+        VMEM((rhs, high * block), F32),
+        VMEM((high, rhs, block), F32),
         VMEM((1, block), F32),
         VMEM((count, 1, block), F32),
+        pltpu.SemaphoreType.DMA((7,)),
         pltpu.SemaphoreType.DMA((13,)),
         pltpu.SemaphoreType.DMA((13,)),
     ]
-    vmem = pl.BlockSpec(memory_space=VMEM)
-    smem = pl.BlockSpec(memory_space=SMEM)
-    return pl.pallas_call(
-        functools.partial(kernel, rows, cols),
-        out_shape=[jax.ShapeDtypeStruct((rhs, block), F32)] * 2,
-        in_specs=[vmem, smem, smem, smem, vmem, vmem, vmem],
-        out_specs=[vmem, vmem],
+    hbm = pl.BlockSpec(memory_space=pltpu.HBM)
+    out = pl.pallas_call(
+        functools.partial(kernel, high, low, cols),
+        out_shape=jax.ShapeDtypeStruct((2 * rhs, block), F32),
+        in_specs=[hbm] * 7,
+        out_specs=pl.BlockSpec(memory_space=VMEM),
         scratch_shapes=scratch,
         compiler_params=pltpu.CompilerParams(
-            collective_id=0, has_side_effects=True, vmem_limit_bytes=48 * 1024 * 1024
+            collective_id=0, has_side_effects=True
         ),
         name="deflated_cg",
     )(points, inv_scales, amplitude, noise_var, targets, initial, ritz_basis)
+    return out[:rhs], out[rhs:]
 
 
 def solution(mesh):
     spread = P(None, ("col", "row"))
+    rows, cols = mesh.shape["row"], mesh.shape["col"]
+    low = next(d for d in range(1, rows + 1) if rows % d == 0 and d * cols >= rows // d)
     return jax.shard_map(
-        functools.partial(local, mesh.shape["row"], mesh.shape["col"]),
+        functools.partial(local, rows // low, low, cols),
         mesh=mesh,
         in_specs=(spread, P(), P(), P(), spread, spread, spread),
         out_specs=(spread, spread),

time: 51.7 us -> 46.6 us (0.901)
  local copies, waits for them, and re-layouts: 4.01 us -> 1.28 us
  Pallas kernels: 45.4 us -> 43.1 us
    unnamed x12 -> x0, local copies, waits for them, and re-layouts: 4.01 us -> none
    pallas_call x1, Pallas kernels: 45.4 us -> 43.1 us  [local(): pl.pallas_call(functools.partial(kernel, high, low, cols), out_shape=jax....]
    slice x0 -> x1, local copies, waits for them, and re-layouts: none -> 1.28 us  [local(): return (out[:rhs], out[rhs:])]
where the time goes in v2:
time: 46.6 us; the launch traced here: 46.3 us
  Pallas kernels  43.1 us (92%)
  between operations  1.93 us (4%)
  local copies, waits for them, and re-layouts  1.28 us (3%)
    pallas_call x1, Pallas kernels, local(): pl.pallas_call(functools.partial(kernel, high, low, cols), out_shape=jax....  43.1 us
    slice x1, local copies, waits for them, and re-layouts, local(): return (out[:rhs], out[rhs:])  1.28 us

profile of v2, /device:TPU:0, one launch (start us, length us, event | category | flops | bytes accessed | tf_op | source)
XLA Modules:
  0.0 46.3 jit_solution(12318795790021939993)
XLA Ops:
  1.9 43.1 %deflated_cg.1 = f32[16,128]{1,0:T(8,128)} custom-call(f32[16,128]{1,0:T(8,128)} %pts_in.1, f32[16]{0:T(128)} %scl_in.1, f32[1]{0:T(128)S(6)} %copy.9.amp_in, f32[1]{0:T(128)S(6)} %copy.10.nug_in, f32[8,128]{1,0:T(8,128)} %tgt_in.1, f32[8,128]{1,0:T(8,128)} %x0_in.1, f32[64,128]{1,0:T(8,128)} %w_in.1), custom_call_target="tpu_custom_call" | custom-call | tf_op jit(solution)/shard_map/deflated_cg/pallas_call | solution.py:302
  45.1 1.3 %fusion = (f32[8,128]{1,0:T(8,128)}, f32[8,128]{1,0:T(8,128)}) fusion(f32[16,128]{1,0:T(8,128)} %deflated_cg.1), kind=kLoop, calls=%fused_computation | loop fusion | bytes 16384 | tf_op jit(solution)/shard_map/slice | solution.py:313

commit v3 on v2

--- a/solution.py
+++ b/solution.py
@@ -101,8 +101,6 @@
 
     each(high, lambda k: greet(col_peer(k)))
     each(rows, lambda k: greet(row_peer(k)))
-    pscr[...] = jnp.zeros_like(pscr)
-    agscr[...] = jnp.zeros_like(agscr)
     for fetch in fetches:
         fetch.wait()
     xj[:, lanes(j)] = pts[...]
@@ -151,7 +149,6 @@
     ts[...] = dot(vj[...], kt[...])
     ts[pl.ds(0, ritz), lanes(h)] += nugget * w[...]
     ts[pl.ds(ritz, rhs), lanes(h)] += nugget * x0[...] - tgt[...]
-    each(high, lambda k: start(5, ts.at[:, lanes(lax.rem(h + k, high))], rs1.at[h], col_peer(k)))
     drain_wi.wait_recv()
     gram = dot(wi[...], ts[...], ((1,), (1,)))
     part = ritz // rows
@@ -162,6 +159,7 @@
         start(6, pscr.at[lax.rem(j + k, rows)], r1.at[me], any_peer(k))
 
     each(count, send_part)
+    each(high, lambda k: start(5, ts.at[:, lanes(lax.rem(h + k, high))], rs1.at[h], col_peer(k)))
     r1[me] = pscr[j]
     rs1[h] = ts[:, lanes(h)]
     drain_r1 = drain(6, r1.at[pl.ds(0, count - 1)])
@@ -187,27 +185,36 @@
     for i in range(ritz // 8):
         top = full[8 * i:8 * i + 8]
         tiles.append(jnp.where(lane < ritz, 0.5 * (top + flipped[8 * i:8 * i + 8]), top))
-    for k in range(ritz):
+    for k in range(0, ritz, 2):
         hold, inner = divmod(k, 8)
-        pivot_row = tiles[hold][inner:inner + 1]
-        inverse = 1.0 / pivot_row[:, k:k + 1]
-        pivot_row = jnp.where(lane_row == k, 1.0, pivot_row) * inverse
+        upper = tiles[hold][inner:inner + 1]
+        lower = tiles[hold][inner + 1:inner + 2]
+        a, b = upper[:, k:k + 1], upper[:, k + 1:k + 2]
+        d, e = lower[:, k:k + 1], lower[:, k + 1:k + 2]
+        inverse = 1.0 / (a * e - b * d)
+        first, second = lane_row == k, lane_row == k + 1
+        upper = jnp.where(first, 1.0, jnp.where(second, 0.0, upper))
+        lower = jnp.where(first, 0.0, jnp.where(second, 1.0, lower))
+        upper, lower = (e * inverse) * upper - (b * inverse) * lower, (a * inverse) * lower - (d * inverse) * upper
         for i in range(ritz // 8):
-            column = jnp.broadcast_to(tiles[i][:, k:k + 1], (8, block))
-            kept = jnp.where(lane == k, 0.0, tiles[i])
+            left = jnp.broadcast_to(tiles[i][:, k:k + 1], (8, block))
+            right = jnp.broadcast_to(tiles[i][:, k + 1:k + 2], (8, block))
+            kept = jnp.where((lane == k) | (lane == k + 1), 0.0, tiles[i])
             if i == hold:
-                column = jnp.where(sub == inner, -1.0, column)
-                kept = jnp.where(sub == inner, 0.0, kept)
-            tiles[i] = kept - column * pivot_row
+                pivots = (sub == inner) | (sub == inner + 1)
+                left = jnp.where(pivots, jnp.where(sub == inner, -1.0, 0.0), left)
+                right = jnp.where(pivots, jnp.where(sub == inner, 0.0, -1.0), right)
+                kept = jnp.where(pivots, 0.0, kept)
+            tiles[i] = (kept - left * upper) - right * lower
     turned = jnp.concatenate(tiles + [pad], axis=0).T
     inverse = turned[:ritz, :ritz]
     amounts = -turned[ritz:ritz + rhs, :ritz]
     moved = dot(amounts, jnp.concatenate([image, w[...]], axis=1))
     residual = -own[ritz:] - moved[:, :block]
     iterate = x0[...] + moved[:, block:]
-    agscr[...] = jnp.concatenate(
-        [dot(residual, image, ((1,), (1,))), jnp.zeros((rhs, block - ritz), F32)], axis=1
-    )
+    against = dot(residual, image, ((1,), (1,)))
+    packed = agscr.shape[0]
+    agscr[...] = jnp.concatenate([against[i:i + packed] for i in range(0, rhs, packed)], axis=1)
     res[...] = residual
     rj[:, lanes(j)] = residual
     ri[:, lanes(h)] = residual
@@ -219,7 +226,8 @@
     drain_rj = drain(8, rj.at[:, others_j])
     drain_ri = drain(9, ri.at[:, others_i])
     drain_ag.wait_recv()
-    against = jnp.sum(ag[...], axis=0)[:, :ritz]
+    against = jnp.sum(ag[...], axis=0)
+    against = jnp.concatenate([against[:, i:i + ritz] for i in range(0, block, ritz)], axis=0)
     weights = dot(against, inverse)
     drain_rj.wait_recv()
     direction_j = rj[...] - dot(weights, vj[pl.ds(0, ritz), :])
@@ -265,6 +273,7 @@
     count = high * rows
     vectors = rhs + ritz
     part = ritz // rows
+    packed = rhs * ritz // block
     scratch = [
         VMEM((feat, block), F32),
         SMEM((feat,), F32),
@@ -287,8 +296,8 @@
         VMEM((part, block), F32),
         VMEM((rhs, rows * block), F32),
         VMEM((rhs, high * block), F32),
-        VMEM((rhs, block), F32),
-        VMEM((count, rhs, block), F32),
+        VMEM((packed, block), F32),
+        VMEM((count, packed, block), F32),
         VMEM((rhs, high * block), F32),
         VMEM((rhs, high * block), F32),
         VMEM((high, rhs, block), F32),

time: 46.6 us -> 48.2 us (1.034)
  Pallas kernels: 43.1 us -> 44.7 us
    pallas_call x1, Pallas kernels: 43.1 us -> 44.7 us  [local(): pl.pallas_call(functools.partial(kernel, high, low, cols), out_shape=jax....]
where the time goes in v3:
time: 48.2 us; the launch traced here: 47.9 us
  Pallas kernels  44.7 us (93%)
  between operations  1.93 us (4%)
  local copies, waits for them, and re-layouts  1.28 us (3%)
    pallas_call x1, Pallas kernels, local(): pl.pallas_call(functools.partial(kernel, high, low, cols), out_shape=jax....  44.7 us
    slice x1, local copies, waits for them, and re-layouts, local(): return (out[:rhs], out[rhs:])  1.28 us

profile of v3, /device:TPU:0, one launch (start us, length us, event | category | flops | bytes accessed | tf_op | source)
XLA Modules:
  0.0 47.9 jit_solution(15943538540084870454)
XLA Ops:
  1.9 44.7 %deflated_cg.1 = f32[16,128]{1,0:T(8,128)} custom-call(f32[16,128]{1,0:T(8,128)} %pts_in.1, f32[16]{0:T(128)} %scl_in.1, f32[1]{0:T(128)S(6)} %copy.9.amp_in, f32[1]{0:T(128)S(6)} %copy.10.nug_in, f32[8,128]{1,0:T(8,128)} %tgt_in.1, f32[8,128]{1,0:T(8,128)} %x0_in.1, f32[64,128]{1,0:T(8,128)} %w_in.1), custom_call_target="tpu_custom_call" | custom-call | tf_op jit(solution)/shard_map/deflated_cg/pallas_call | solution.py:311
  46.6 1.3 %fusion = (f32[8,128]{1,0:T(8,128)}, f32[8,128]{1,0:T(8,128)}) fusion(f32[16,128]{1,0:T(8,128)} %deflated_cg.1), kind=kLoop, calls=%fused_computation | loop fusion | bytes 16384 | tf_op jit(solution)/shard_map/slice | solution.py:322

commit v4 on v3

--- a/solution.py
+++ b/solution.py
@@ -185,27 +185,26 @@
     for i in range(ritz // 8):
         top = full[8 * i:8 * i + 8]
         tiles.append(jnp.where(lane < ritz, 0.5 * (top + flipped[8 * i:8 * i + 8]), top))
-    for k in range(0, ritz, 2):
-        hold, inner = divmod(k, 8)
-        upper = tiles[hold][inner:inner + 1]
-        lower = tiles[hold][inner + 1:inner + 2]
-        a, b = upper[:, k:k + 1], upper[:, k + 1:k + 2]
-        d, e = lower[:, k:k + 1], lower[:, k + 1:k + 2]
-        inverse = 1.0 / (a * e - b * d)
-        first, second = lane_row == k, lane_row == k + 1
-        upper = jnp.where(first, 1.0, jnp.where(second, 0.0, upper))
-        lower = jnp.where(first, 0.0, jnp.where(second, 1.0, lower))
-        upper, lower = (e * inverse) * upper - (b * inverse) * lower, (a * inverse) * lower - (d * inverse) * upper
-        for i in range(ritz // 8):
-            left = jnp.broadcast_to(tiles[i][:, k:k + 1], (8, block))
-            right = jnp.broadcast_to(tiles[i][:, k + 1:k + 2], (8, block))
-            kept = jnp.where((lane == k) | (lane == k + 1), 0.0, tiles[i])
-            if i == hold:
-                pivots = (sub == inner) | (sub == inner + 1)
-                left = jnp.where(pivots, jnp.where(sub == inner, -1.0, 0.0), left)
-                right = jnp.where(pivots, jnp.where(sub == inner, 0.0, -1.0), right)
-                kept = jnp.where(pivots, 0.0, kept)
-            tiles[i] = (kept - left * upper) - right * lower
+    wide = 8
+    for base in range(0, ritz, wide):
+        panel = [[jnp.broadcast_to(t[:, k:k + 1], (8, block)) for t in tiles] for k in range(base, base + wide)]
+        for p in range(wide):
+            k = base + p
+            hold, inner = divmod(k, 8)
+            inverse = 1.0 / panel[p][hold][inner:inner + 1]
+            pivot_row = jnp.where(lane_row == k, 1.0, tiles[hold][inner:inner + 1]) * inverse
+            ahead = [panel[q][hold][inner:inner + 1] * inverse for q in range(p + 1, wide)]
+            for i in range(ritz // 8):
+                column = panel[p][i]
+                kept = jnp.where(lane == k, 0.0, tiles[i])
+                later = [panel[q][i] for q in range(p + 1, wide)]
+                if i == hold:
+                    column = jnp.where(sub == inner, -1.0, column)
+                    kept = jnp.where(sub == inner, 0.0, kept)
+                    later = [jnp.where(sub == inner, 0.0, value) for value in later]
+                tiles[i] = kept - column * pivot_row
+                for q, (value, row) in enumerate(zip(later, ahead)):
+                    panel[p + 1 + q][i] = value - column * row
     turned = jnp.concatenate(tiles + [pad], axis=0).T
     inverse = turned[:ritz, :ritz]
     amounts = -turned[ritz:ritz + rhs, :ritz]

time: 48.2 us -> 40.8 us (0.85)
  Pallas kernels: 44.7 us -> 37.3 us
    pallas_call x1, Pallas kernels: 44.7 us -> 37.3 us  [local(): pl.pallas_call(functools.partial(kernel, high, low, cols), out_shape=jax....]
where the time goes in v4:
time: 40.8 us; the launch traced here: 40.5 us
  Pallas kernels  37.3 us (91%)
  between operations  1.93 us (5%)
  local copies, waits for them, and re-layouts  1.28 us (3%)
    pallas_call x1, Pallas kernels, local(): pl.pallas_call(functools.partial(kernel, high, low, cols), out_shape=jax....  37.3 us
    slice x1, local copies, waits for them, and re-layouts, local(): return (out[:rhs], out[rhs:])  1.28 us

profile of v4, /device:TPU:0, one launch (start us, length us, event | category | flops | bytes accessed | tf_op | source)
XLA Modules:
  0.0 40.5 jit_solution(10880942170631217645)
XLA Ops:
  1.9 37.3 %deflated_cg.1 = f32[16,128]{1,0:T(8,128)} custom-call(f32[16,128]{1,0:T(8,128)} %pts_in.1, f32[16]{0:T(128)} %scl_in.1, f32[1]{0:T(128)S(6)} %copy.9.amp_in, f32[1]{0:T(128)S(6)} %copy.10.nug_in, f32[8,128]{1,0:T(8,128)} %tgt_in.1, f32[8,128]{1,0:T(8,128)} %x0_in.1, f32[64,128]{1,0:T(8,128)} %w_in.1), custom_call_target="tpu_custom_call" | custom-call | tf_op jit(solution)/shard_map/deflated_cg/pallas_call | solution.py:310
  39.3 1.3 %fusion = (f32[8,128]{1,0:T(8,128)}, f32[8,128]{1,0:T(8,128)}) fusion(f32[16,128]{1,0:T(8,128)} %deflated_cg.1), kind=kLoop, calls=%fused_computation | loop fusion | bytes 16384 | tf_op jit(solution)/shard_map/slice | solution.py:321
